TPU v7x, 32 devices: a whole 2x2x4 slice. The times are simulated.
32 devices in a mesh: seq: 8 (over z, x), tp: 4 (over y, core).
Axes of the slice: x: 2, y: 2, z: 4, core: 2. Of those that a mesh axis runs over, the one named last changes fastest.
Arguments:
- tokens: bfloat16 [1024, 4608], P('seq'), may hold values from -6 to 6
- counts: int32 [8], P('seq'), may hold values from 0 to 32, as said below
- selected: int32 [8, 32], P('seq'), may hold values from 0 to 127, as said below
- router_w: float32 [4608], replicated, may hold values from -0.09375 to 0.09375
- pre_gain: float32 [4608], replicated, may hold values from 0.25 to 1.75
- post_gain: float32 [4608], replicated, may hold values from 0.25 to 1.75
- gate_w: bfloat16 [4608, 36864], P(None, ('seq', 'tp')), may hold values from -0.09375 to 0.09375
- up_w: bfloat16 [4608, 36864], P(None, ('seq', 'tp')), may hold values from -0.09375 to 0.09375
- down_w: bfloat16 [36864, 4608], P(('seq', 'tp')), may hold values from -0.0625 to 0.0625
Outputs:
- layer_out: bfloat16 [1024, 4608], P('seq')
Inputs may be any that keep to these rules, and one draw needn't show every extreme that they name: The counts sum to 128. For every shard s, the sum of the counts of the shards before s differs from s * 16 by at most 32. Each shard's first counts entries are distinct token positions of that shard in increasing order; the entries after them are padding and name no selected token.
All inputs are finite; a program needn't handle non-finite values.
Results may differ from a plain program's by a relative error of at most 0.003.
Values may be sent and summed in bfloat16 or wider, within the bound.
A program may use at most 128 MiB of HBM per device.

v0:
```python
import functools

import jax
import jax.numpy as jnp
from jax import lax
from jax.experimental import pallas as pl
from jax.experimental.pallas import tpu as pltpu
from jax.sharding import PartitionSpec as P

EPS = 1e-06
MESH = pl.DeviceIdType.MESH
VMEM_BYTES = 67_043_328


def norm_rows(values, scale_vec):
    return values * lax.rsqrt(jnp.mean(values * values, axis=-1, keepdims=True) + EPS) * scale_vec


def pick_t(sel_ref, count, tok_rows):
    cap = sel_ref.shape[1]
    pos = lax.broadcasted_iota(jnp.int32, (tok_rows, cap), 0)
    slot = lax.broadcasted_iota(jnp.int32, (tok_rows, cap), 1)
    hit = (pos == sel_ref[...]) & (slot < count)
    return jnp.where(hit, 1.0, 0.0)


def dot_t(a, b):
    return jnp.dot(a.T.astype(jnp.bfloat16), b, preferred_element_type=jnp.float32)


def main_kernel(
    dims, cnt_ref, sel_ref, gain_ref, router_ref, tok_hbm, gate_hbm, up_hbm, down_hbm, out_ref, weight_ref,
    tok, gw, uw, dw, rows, cbuf, esrc, edst, xb, gacc, uacc, hid,
    sb, ra, own, ch, rb, plf, pz, rc, win, outb,
    tok_sem, w_sem, send, recv,
):
    seq, tp, cap, load, quarter, pieces = dims
    nz = seq // 2
    reach = cap // load
    blocks = 2 * reach + 1
    width = blocks * load
    tok_rows = tok.shape[0]
    s = lax.axis_index("seq")
    t = lax.axis_index("tp")
    z, x = lax.div(s, 2), lax.rem(s, 2)
    y, c = lax.div(t, 2), lax.rem(t, 2)
    xpeer = z * 2 + (1 - x)
    ypeer = (1 - y) * 2 + c
    mate = y * 2 + (1 - c)
    far = (1 - y) * 2 + (1 - c)

    tok_copy = pltpu.make_async_copy(tok_hbm, tok, tok_sem)
    tok_copy.start()
    barrier = pltpu.get_barrier_semaphore()
    peers = [(lax.rem(s + d, seq), t) for d in range(1, seq)]
    peers += [(s, ypeer), (s, mate), (xpeer, ypeer)]
    for peer in peers:
        pl.semaphore_signal(barrier, inc=1, device_id=peer, device_id_type=MESH)
    gate_up, down = [], []
    for i, (src, dst) in enumerate(((gate_hbm, gw), (up_hbm, uw), (down_hbm, dw))):
        step = src.shape[0] // 4
        for j in range(4):
            part = pl.ds(j * step, step)
            copy = pltpu.make_async_copy(src.at[part], dst.at[part], w_sem.at[i * 4 + j])
            copy.start()
            (gate_up if i < 2 else down).append(copy)

    used = [0]

    def remote(src, dst, peer):
        k = used[0]
        used[0] += 1
        copy = pltpu.make_async_remote_copy(
            src_ref=src, dst_ref=dst, send_sem=send.at[k], recv_sem=recv.at[k],
            device_id=peer, device_id_type=MESH,
        )
        copy.start()
        return copy

    count = cnt_ref[0]
    cbuf[s] = jnp.full(cbuf.shape[1:], count, jnp.int32)
    pl.semaphore_wait(barrier, len(peers))
    counted = [remote(cbuf.at[s], cbuf.at[s], (lax.rem(s + d, seq), t)) for d in range(1, seq)]

    tok_copy.wait()
    compact = dot_t(pick_t(sel_ref, count, tok_rows), tok[...])
    rows[...] = compact
    inv = lax.rsqrt(jnp.mean(compact * compact, axis=-1, keepdims=True) + EPS)
    columns = pl.ds(pl.multiple_of(t * quarter, 128), quarter)
    normed = (rows[:, columns] * inv * gain_ref[:, columns]).astype(jnp.bfloat16)
    for copy in counted:
        copy.wait()
    start = jnp.zeros(cbuf.shape[1:], jnp.int32)
    for i in range(seq):
        start = start + cbuf[i] * (i < s).astype(jnp.int32)
    slot = lax.broadcasted_iota(jnp.int32, (cap, width), 0)
    at = lax.broadcasted_iota(jnp.int32, (cap, width), 1) + (s - reach) * load
    take = jnp.where((start[:1, :width] + slot == at) & (slot < count), 1.0, 0.0)

    esrc[...] = dot_t(take, normed).astype(jnp.bfloat16).reshape(blocks, load, quarter)
    near = []
    for d in range(-reach, reach + 1):
        if d:
            near.append(remote(esrc.at[reach + d], edst.at[len(near)], (lax.rem(s + d + seq, seq), t)))
    weight = jax.nn.sigmoid(jnp.sum(compact * router_ref[...], axis=-1, keepdims=True))
    weight_ref[...] = jnp.broadcast_to(weight, weight_ref.shape)
    block = esrc[reach].astype(jnp.float32)
    for i, copy in enumerate(near):
        copy.wait()
        block = block + edst[i].astype(jnp.float32)
    piece = quarter // pieces
    for p in range(pieces):
        xb[t, p, s] = block[:, p * piece:(p + 1) * piece].astype(jnp.bfloat16)

    rings = [
        [remote(xb.at[t, p, s], xb.at[t, p, s], (lax.rem(s + d, seq), t)) for d in range(1, seq)]
        for p in range(pieces)
    ]
    over_y, over_c, forward = [], [], []
    for p in range(pieces):
        for copy in rings[p]:
            copy.wait()
        over_y.append(remote(xb.at[t, p], xb.at[t, p], (s, ypeer)))
        over_c.append(remote(xb.at[t, p], xb.at[t, p], (s, mate)))
    for copy in gate_up:
        copy.wait()

    def add_piece(q, p, first=False):
        part = pl.ds(pl.multiple_of(q * quarter + p * piece, 128), piece)
        rows_in = xb[q, p].reshape(seq * load, piece)
        g = jnp.dot(rows_in, gw[part, :], preferred_element_type=jnp.float32)
        u = jnp.dot(rows_in, uw[part, :], preferred_element_type=jnp.float32)
        if first:
            gacc[...] = g
            uacc[...] = u
        else:
            gacc[...] += g
            uacc[...] += u

    for p in range(pieces):
        add_piece(t, p, p == 0)
        over_y[p].wait()
        forward.append(remote(xb.at[ypeer, p], xb.at[ypeer, p], (s, mate)))
    for p in range(pieces):
        over_c[p].wait()
        add_piece(mate, p)
        add_piece(ypeer, p)
    for p in range(pieces):
        forward[p].wait()
        add_piece(far, p)
    hid[...] = (jax.nn.gelu(gacc[...], approximate=True) * uacc[...]).astype(jnp.bfloat16)
    for copy in down:
        copy.wait()

    def product(q):
        part = pl.ds(pl.multiple_of(q * quarter, 128), quarter)
        m = jnp.dot(hid[...], dw[:, part], preferred_element_type=jnp.float32)
        return m.reshape(nz, 2, load, quarter)

    def to_mate(k):
        sb[k] = product(k * 2 + (1 - c)).astype(jnp.bfloat16)
        return remote(sb.at[k], ra.at[k], (s, mate))

    def chip_sum(k, copy):
        copy.wait()
        chip = own[k] + ra[k].astype(jnp.float32)
        own[k] = chip
        ch[k] = chip.astype(jnp.bfloat16)

    away = to_mate(1 - y)
    own[1 - y] = product((1 - y) * 2 + c)
    chip_sum(1 - y, away)
    plane = [
        remote(ch.at[1 - y, :, 1 - x], rb.at[2], (xpeer, ypeer)),
        remote(ch.at[1 - y, :, x], rb.at[1], (s, ypeer)),
    ]
    home = to_mate(y)
    own[y] = product(y * 2 + c)
    chip_sum(y, home)
    plane.append(remote(ch.at[y, :, 1 - x], rb.at[0], (xpeer, t)))
    for copy in plane:
        copy.wait()
    level = own[y, :, x] + rb[0].astype(jnp.float32) + rb[1].astype(jnp.float32) + rb[2].astype(jnp.float32)
    plf[...] = level
    pz[...] = level.astype(jnp.bfloat16)

    stack = []
    for d in range(1, nz):
        other = lax.rem(z + d, nz)
        stack.append(remote(pz.at[other], rc.at[d - 1], (other * 2 + x, t)))
    mixed = plf[z]
    for d in range(1, nz):
        stack[d - 1].wait()
        mixed = mixed + rc[d - 1].astype(jnp.float32)

    win[reach] = mixed.astype(jnp.bfloat16)
    near = []
    for d in range(-reach, reach + 1):
        if d:
            near.append(remote(win.at[reach], win.at[reach - d], (lax.rem(s + d + seq, seq), t)))
    for copy in near:
        copy.wait()
    outb[t] = jnp.dot(take.astype(jnp.bfloat16), win[...].reshape(width, quarter),
                      preferred_element_type=jnp.float32).astype(jnp.bfloat16)
    last_y = remote(outb.at[t], outb.at[t], (s, ypeer))
    last_c = remote(outb.at[t], outb.at[t], (s, mate))
    last_y.wait()
    last = remote(outb.at[ypeer], outb.at[ypeer], (s, mate))
    last_c.wait()
    last.wait()
    out_ref[...] = outb[...]


def final_kernel(quarters, cnt_ref, sel_ref, gain_ref, tok_ref, mixed_ref, weight_ref, out_ref):
    tok_rows, width = tok_ref.shape
    quarter = width // quarters
    picked = pick_t(sel_ref, cnt_ref[0], tok_rows)
    pick = picked.astype(jnp.bfloat16)
    weight = weight_ref[:, :1]
    square = jnp.zeros_like(weight)
    for q in range(quarters):
        part = mixed_ref[q].astype(jnp.float32)
        square = square + jnp.sum(part * part, axis=-1, keepdims=True)
    inv = lax.rsqrt(square / width + EPS)
    for q in range(quarters):
        cols = slice(q * quarter, (q + 1) * quarter)
        update = weight * (mixed_ref[q].astype(jnp.float32) * inv * gain_ref[:, cols])
        high = update.astype(jnp.bfloat16)
        low = (update - high.astype(jnp.float32)).astype(jnp.bfloat16)
        moved = jnp.dot(pick, high, preferred_element_type=jnp.float32)
        moved = moved + jnp.dot(pick, low, preferred_element_type=jnp.float32)
        out_ref[:, cols] = (tok_ref[:, cols].astype(jnp.float32) + moved).astype(jnp.bfloat16)


def fused_body(tokens, counts, selected, router_w, pre_gain, post_gain, gate_w, up_w, down_w):
    seq, tp = lax.axis_size("seq"), lax.axis_size("tp")
    tok_rows, width = tokens.shape
    cap = selected.shape[1]
    load = cap // 2
    total = seq * load
    hidden = gate_w.shape[1]
    quarter = width // tp
    nz = seq // 2
    reach = cap // load
    bf16, f32 = jnp.bfloat16, jnp.float32
    pieces = 3 if quarter % 384 == 0 else 1
    copies = (seq - 1) * (1 + pieces) + 3 * pieces + 2 + 3 + (nz - 1) + 4 * reach + 3
    vmem = pl.BlockSpec(memory_space=pltpu.VMEM)
    smem = pl.BlockSpec(memory_space=pltpu.SMEM)
    anywhere = pl.BlockSpec(memory_space=pl.ANY)
    mixed, weight = pl.pallas_call(
        functools.partial(main_kernel, (seq, tp, cap, load, quarter, pieces)),
        out_shape=(
            jax.ShapeDtypeStruct((tp, cap, quarter), bf16),
            jax.ShapeDtypeStruct((cap, 128), f32),
        ),
        in_specs=[smem, vmem, vmem, vmem] + [anywhere] * 4,
        out_specs=(vmem, vmem),
        scratch_shapes=[
            pltpu.VMEM((tok_rows, width), bf16),
            pltpu.VMEM((width, hidden), bf16),
            pltpu.VMEM((width, hidden), bf16),
            pltpu.VMEM((hidden, width), bf16),
            pltpu.VMEM((cap, width), f32),
            pltpu.VMEM((seq, 8, 128), jnp.int32),
            pltpu.VMEM((2 * reach + 1, load, quarter), bf16),
            pltpu.VMEM((2 * reach, load, quarter), bf16),
            pltpu.VMEM((tp, pieces, seq, load, quarter // pieces), bf16),
            pltpu.VMEM((total, hidden), f32),
            pltpu.VMEM((total, hidden), f32),
            pltpu.VMEM((total, hidden), bf16),
            pltpu.VMEM((2, nz, 2, load, quarter), bf16),
            pltpu.VMEM((2, nz, 2, load, quarter), bf16),
            pltpu.VMEM((2, nz, 2, load, quarter), f32),
            pltpu.VMEM((2, nz, 2, load, quarter), bf16),
            pltpu.VMEM((3, nz, load, quarter), bf16),
            pltpu.VMEM((nz, load, quarter), f32),
            pltpu.VMEM((nz, load, quarter), bf16),
            pltpu.VMEM((nz - 1, load, quarter), bf16),
            pltpu.VMEM((2 * reach + 1, load, quarter), bf16),
            pltpu.VMEM((tp, cap, quarter), bf16),
            pltpu.SemaphoreType.DMA,
            pltpu.SemaphoreType.DMA((12,)),
            pltpu.SemaphoreType.DMA((copies,)),
            pltpu.SemaphoreType.DMA((copies,)),
        ],
        compiler_params=pltpu.CompilerParams(
            collective_id=0, has_side_effects=True, vmem_limit_bytes=VMEM_BYTES - (4 << 20)
        ),
    )(counts, selected, pre_gain[None], router_w[None], tokens, gate_w, up_w, down_w)
    return pl.pallas_call(
        functools.partial(final_kernel, tp),
        out_shape=jax.ShapeDtypeStruct(tokens.shape, tokens.dtype),
        in_specs=[smem] + [vmem] * 5,
        out_specs=vmem,
    )(counts, selected, post_gain[None], tokens, mixed, weight)


def spread_body(tokens, counts, selected, router_w, pre_gain, post_gain, gate_w, up_w, down_w):
    tok_rows = tokens.shape[0]
    capacity = selected.shape[1]
    pair_count = lax.axis_size("tp")
    own_count = counts[0]
    chosen = selected[0]
    is_live = jnp.arange(capacity) < own_count
    positions = jnp.arange(tok_rows)
    picker = ((chosen[:, None] == positions[None, :]) & is_live[:, None]).astype(jnp.bfloat16)
    compact = jnp.dot(picker, tokens, preferred_element_type=jnp.float32).astype(jnp.bfloat16)
    piece_rows = compact.shape[0] // pair_count
    tp_index = lax.axis_index("tp")
    rows_float = compact.astype(jnp.float32)
    weight = jax.nn.sigmoid(jnp.dot(rows_float, router_w, precision=lax.Precision.HIGHEST))
    normed = norm_rows(rows_float, pre_gain).astype(jnp.bfloat16)
    segment = lax.all_gather(normed, "seq", axis=0, tiled=True)
    gate_part = jnp.dot(segment, gate_w, preferred_element_type=jnp.float32)
    up_part = jnp.dot(segment, up_w, preferred_element_type=jnp.float32)
    hidden = (jax.nn.gelu(gate_part, approximate=True) * up_part).astype(jnp.bfloat16)
    mixed = lax.psum_scatter(
        jnp.dot(hidden, down_w, preferred_element_type=jnp.float32),
        ("seq", "tp"),
        scatter_dimension=0,
        tiled=True,
    )
    own_weight = lax.dynamic_slice_in_dim(weight, tp_index * piece_rows, piece_rows, 0)
    finished = own_weight[:, None] * norm_rows(mixed, post_gain)
    updates = lax.all_gather(finished.astype(jnp.bfloat16), "tp", axis=0, tiled=True).astype(
        finished.dtype
    )
    scattered = jnp.einsum(
        "ct,cd->td", picker.astype(jnp.float32), updates, precision=lax.Precision.HIGHEST
    )
    return (tokens.astype(jnp.float32) + scattered).astype(jnp.bfloat16)


def body(*args):
    tokens, selected, gate_w = args[0], args[2], args[6]
    seq, tp = lax.axis_size("seq"), lax.axis_size("tp")
    load, hidden, width = selected.shape[1] // 2, gate_w.shape[1], tokens.shape[1]
    fits = (
        tp == 4 and seq % 2 == 0 and seq > 5 and load % 16 == 0 and 5 * load <= 128 and (seq * load) % 128 == 0
        and width % (tp * 128) == 0 and hidden % 128 == 0
        and 6 * width * hidden + 24 * seq * load * width < VMEM_BYTES
    )
    return fused_body(*args) if fits else spread_body(*args)


def solution(mesh):
    in_specs = (
        P("seq", None),
        P("seq"),
        P("seq", None),
        P(),
        P(),
        P(),
        P(None, ("seq", "tp")),
        P(None, ("seq", "tp")),
        P(("seq", "tp"), None),
    )
    out_specs = P("seq", None)
    return jax.shard_map(body, mesh=mesh, in_specs=in_specs, out_specs=out_specs, check_vma=False)
```

profile of v0, /device:TPU:0, one launch (start us, length us, event | category | flops | bytes accessed | tf_op | source)
XLA Modules:
  0.0 66.4 jit_solution(1486935990320132593)
XLA Ops:
  0.7 1.3 %broadcast_in_dim.11.router_ref = f32[1,4608]{1,0:T(1,128)} reshape(f32[4608]{0:T(1024)} %param.12) | data formatting | bytes 36864 | tf_op jit(solution)/shard_map/broadcast_in_dim | solution.py:290
  2.0 1.3 %broadcast_in_dim.10.gain_ref = f32[1,4608]{1,0:T(1,128)} reshape(f32[4608]{0:T(1024)} %param.13) | data formatting | bytes 36864 | tf_op jit(solution)/shard_map/broadcast_in_dim | solution.py:290
  3.3 1.3 %broadcast_in_dim.9.gain_ref = f32[1,4608]{1,0:T(1,128)} reshape(f32[4608]{0:T(1024)} %param.14) | data formatting | bytes 36864 | tf_op jit(solution)/shard_map/broadcast_in_dim | solution.py:296
  4.7 58.4 %shard_map.91 = (bf16[4,32,1152]{2,1,0:T(8,128)(2,1)}, f32[32,128]{1,0:T(8,128)}) custom-call(s32[1]{0:T(128)S(6)} %copy.10.cnt_ref, s32[1,32]{1,0:T(1,128)} %sel_ref.3, f32[1,4608]{1,0:T(1,128)} %broadcast_in_dim.10.gain_ref, f32[1,4608]{1,0:T(1,128)} %broadcast_in_dim.11.router_ref, bf16[128,4608]{1,0:T(8,128)(2,1)} %tok_ref.1, ...), custom_call_target="tpu_custom_call" | custom-call | tf_op jit(solution)/shard_map/pallas_call | solution.py:251
  63.1 3.3 %shard_map.92 = bf16[128,4608]{1,0:T(8,128)(2,1)} custom-call(s32[1]{0:T(128)S(6)} %copy.10.cnt_ref, s32[1,32]{1,0:T(1,128)} %sel_ref.3, f32[1,4608]{1,0:T(1,128)} %broadcast_in_dim.9.gain_ref, bf16[128,4608]{1,0:T(8,128)(2,1)} %tok_ref.1, bf16[4,32,1152]{2,1,0:T(8,128)(2,1)} %get-tuple-element.7.mixed_ref, f32[32,128]{1,0:T(8,128)} %get-tuple-element.8.weight_ref), custom_call_target="tpu_custom_call" | custom-call | tf_op jit(solution)/shard_map/pallas_call | solution.py:291
where the time goes:
time: 66.8 us; the launch traced here: 66.4 us
  Pallas kernels  61.7 us (92%)
  local copies, waits for them, and re-layouts  4.02 us (6%)
    pallas_call x1, Pallas kernels, fused_body(): pl.pallas_call(functools.partial(main_kernel, (seq, tp, cap, load, quarte...  58.4 us
    pallas_call x1, Pallas kernels, fused_body(): pl.pallas_call(functools.partial(final_kernel, tp), out_shape=jax.ShapeDt...  3.33 us
    broadcast_in_dim x1, local copies, waits for them, and re-layouts, fused_body(): pre_gain[None]  1.35 us
    broadcast_in_dim x1, local copies, waits for them, and re-layouts, fused_body(): post_gain[None]  1.34 us
    broadcast_in_dim x1, local copies, waits for them, and re-layouts, fused_body(): router_w[None]  1.34 us

commit v1 on v0

--- a/solution.py
+++ b/solution.py
@@ -24,15 +24,19 @@
     return jnp.where(hit, 1.0, 0.0)
 
 
+def vec_row(vecs, which, first, count):
+    return jnp.concatenate([vecs[which, pl.ds(first + k, 1), :] for k in range(count)], axis=1)
+
+
 def dot_t(a, b):
     return jnp.dot(a.T.astype(jnp.bfloat16), b, preferred_element_type=jnp.float32)
 
 
 def main_kernel(
-    dims, cnt_ref, sel_ref, gain_ref, router_ref, tok_hbm, gate_hbm, up_hbm, down_hbm, out_ref, weight_ref,
-    tok, gw, uw, dw, rows, cbuf, esrc, edst, xb, gacc, uacc, hid,
+    dims, cnt_ref, sel_hbm, gain_hbm, router_hbm, post_hbm, tok_hbm, gate_hbm, up_hbm, down_hbm, out_ref,
+    tok, gw, uw, dw, rows, sel_ref, vecs, cbuf, esrc, edst, xb, gacc, uacc, hid,
     sb, ra, own, ch, rb, plf, pz, rc, win, outb,
-    tok_sem, w_sem, send, recv,
+    tok_sem, v_sem, w_sem, send, recv,
 ):
     seq, tp, cap, load, quarter, pieces = dims
     nz = seq // 2
@@ -51,6 +55,11 @@
 
     tok_copy = pltpu.make_async_copy(tok_hbm, tok, tok_sem)
     tok_copy.start()
+    small = [pltpu.make_async_copy(sel_hbm, sel_ref, v_sem.at[0])]
+    for i, src in enumerate((gain_hbm, router_hbm, post_hbm)):
+        small.append(pltpu.make_async_copy(src, vecs.at[i], v_sem.at[i + 1]))
+    for copy in small:
+        copy.start()
     barrier = pltpu.get_barrier_semaphore()
     peers = [(lax.rem(s + d, seq), t) for d in range(1, seq)]
     peers += [(s, ypeer), (s, mate), (xpeer, ypeer)]
@@ -82,12 +91,16 @@
     pl.semaphore_wait(barrier, len(peers))
     counted = [remote(cbuf.at[s], cbuf.at[s], (lax.rem(s + d, seq), t)) for d in range(1, seq)]
 
+    for copy in small:
+        copy.wait()
     tok_copy.wait()
     compact = dot_t(pick_t(sel_ref, count, tok_rows), tok[...])
     rows[...] = compact
     inv = lax.rsqrt(jnp.mean(compact * compact, axis=-1, keepdims=True) + EPS)
     columns = pl.ds(pl.multiple_of(t * quarter, 128), quarter)
-    normed = (rows[:, columns] * inv * gain_ref[:, columns]).astype(jnp.bfloat16)
+    lanes = quarter // 128
+    gain = vec_row(vecs, 0, t * lanes, lanes)
+    normed = (rows[:, columns] * inv * gain).astype(jnp.bfloat16)
     for copy in counted:
         copy.wait()
     start = jnp.zeros(cbuf.shape[1:], jnp.int32)
@@ -102,8 +115,8 @@
     for d in range(-reach, reach + 1):
         if d:
             near.append(remote(esrc.at[reach + d], edst.at[len(near)], (lax.rem(s + d + seq, seq), t)))
-    weight = jax.nn.sigmoid(jnp.sum(compact * router_ref[...], axis=-1, keepdims=True))
-    weight_ref[...] = jnp.broadcast_to(weight, weight_ref.shape)
+    router = vec_row(vecs, 1, 0, compact.shape[1] // 128)
+    weight = jax.nn.sigmoid(jnp.sum(compact * router, axis=-1, keepdims=True))
     block = esrc[reach].astype(jnp.float32)
     for i, copy in enumerate(near):
         copy.wait()
@@ -208,28 +221,25 @@
     last = remote(outb.at[ypeer], outb.at[ypeer], (s, mate))
     last_c.wait()
     last.wait()
-    out_ref[...] = outb[...]
-
-
-def final_kernel(quarters, cnt_ref, sel_ref, gain_ref, tok_ref, mixed_ref, weight_ref, out_ref):
-    tok_rows, width = tok_ref.shape
-    quarter = width // quarters
-    picked = pick_t(sel_ref, cnt_ref[0], tok_rows)
-    pick = picked.astype(jnp.bfloat16)
-    weight = weight_ref[:, :1]
-    square = jnp.zeros_like(weight)
-    for q in range(quarters):
-        part = mixed_ref[q].astype(jnp.float32)
-        square = square + jnp.sum(part * part, axis=-1, keepdims=True)
-    inv = lax.rsqrt(square / width + EPS)
-    for q in range(quarters):
-        cols = slice(q * quarter, (q + 1) * quarter)
-        update = weight * (mixed_ref[q].astype(jnp.float32) * inv * gain_ref[:, cols])
+    parts = [outb[q].astype(jnp.float32) for q in range(outb.shape[0])]
+    square = sum(jnp.sum(part * part, axis=-1, keepdims=True) for part in parts)
+    scale = lax.rsqrt(square / compact.shape[1] + EPS)
+    for q, part in enumerate(parts):
+        update = weight * (part * scale * vec_row(vecs, 2, q * lanes, lanes))
         high = update.astype(jnp.bfloat16)
         low = (update - high.astype(jnp.float32)).astype(jnp.bfloat16)
-        moved = jnp.dot(pick, high, preferred_element_type=jnp.float32)
-        moved = moved + jnp.dot(pick, low, preferred_element_type=jnp.float32)
-        out_ref[:, cols] = (tok_ref[:, cols].astype(jnp.float32) + moved).astype(jnp.bfloat16)
+        pick = pick_t(sel_ref, count, tok_rows).astype(jnp.bfloat16)
+        both = jnp.concatenate([pick, pick], axis=1)
+        moved = jnp.dot(both, jnp.concatenate([high, low], axis=0), preferred_element_type=jnp.float32)
+        cols = pl.ds(q * quarter, quarter)
+        out_ref[:, cols] = (tok[:, cols].astype(jnp.float32) + moved).astype(jnp.bfloat16)
+
+
+def final_kernel(cnt_ref, sel_ref, tok_ref, update_ref, out_ref):
+    pick = pick_t(sel_ref, cnt_ref[0], tok_ref.shape[0]).astype(jnp.bfloat16)
+    both = jnp.concatenate([pick, pick], axis=1)
+    moved = jnp.dot(both, update_ref[...], preferred_element_type=jnp.float32)
+    out_ref[...] = (tok_ref[...].astype(jnp.float32) + moved).astype(jnp.bfloat16)
 
 
 def fused_body(tokens, counts, selected, router_w, pre_gain, post_gain, gate_w, up_w, down_w):
@@ -248,20 +258,19 @@
     vmem = pl.BlockSpec(memory_space=pltpu.VMEM)
     smem = pl.BlockSpec(memory_space=pltpu.SMEM)
     anywhere = pl.BlockSpec(memory_space=pl.ANY)
-    mixed, weight = pl.pallas_call(
+    return pl.pallas_call(
         functools.partial(main_kernel, (seq, tp, cap, load, quarter, pieces)),
-        out_shape=(
-            jax.ShapeDtypeStruct((tp, cap, quarter), bf16),
-            jax.ShapeDtypeStruct((cap, 128), f32),
-        ),
-        in_specs=[smem, vmem, vmem, vmem] + [anywhere] * 4,
-        out_specs=(vmem, vmem),
+        out_shape=jax.ShapeDtypeStruct(tokens.shape, bf16),
+        in_specs=[smem] + [anywhere] * 8,
+        out_specs=vmem,
         scratch_shapes=[
             pltpu.VMEM((tok_rows, width), bf16),
             pltpu.VMEM((width, hidden), bf16),
             pltpu.VMEM((width, hidden), bf16),
             pltpu.VMEM((hidden, width), bf16),
             pltpu.VMEM((cap, width), f32),
+            pltpu.VMEM(selected.shape, jnp.int32),
+            pltpu.VMEM((3, width // 128, 128), f32),
             pltpu.VMEM((seq, 8, 128), jnp.int32),
             pltpu.VMEM((2 * reach + 1, load, quarter), bf16),
             pltpu.VMEM((2 * reach, load, quarter), bf16),
@@ -280,6 +289,7 @@
             pltpu.VMEM((2 * reach + 1, load, quarter), bf16),
             pltpu.VMEM((tp, cap, quarter), bf16),
             pltpu.SemaphoreType.DMA,
+            pltpu.SemaphoreType.DMA((4,)),
             pltpu.SemaphoreType.DMA((12,)),
             pltpu.SemaphoreType.DMA((copies,)),
             pltpu.SemaphoreType.DMA((copies,)),
@@ -287,15 +297,10 @@
         compiler_params=pltpu.CompilerParams(
             collective_id=0, has_side_effects=True, vmem_limit_bytes=VMEM_BYTES - (4 << 20)
         ),
-    )(counts, selected, pre_gain[None], router_w[None], tokens, gate_w, up_w, down_w)
-    return pl.pallas_call(
-        functools.partial(final_kernel, tp),
-        out_shape=jax.ShapeDtypeStruct(tokens.shape, tokens.dtype),
-        in_specs=[smem] + [vmem] * 5,
-        out_specs=vmem,
-    )(counts, selected, post_gain[None], tokens, mixed, weight)
-
-
+    )(
+        counts, selected, *(v.reshape(width // 128, 128) for v in (pre_gain, router_w, post_gain)),
+        tokens, gate_w, up_w, down_w,
+    )
 def spread_body(tokens, counts, selected, router_w, pre_gain, post_gain, gate_w, up_w, down_w):
     tok_rows = tokens.shape[0]
     capacity = selected.shape[1]

time: 66.8 us -> 61.8 us (0.925)
  Pallas kernels: 61.7 us -> 58.6 us
  local copies, waits for them, and re-layouts: 4.02 us -> 2.36 us
    broadcast_in_dim x3 -> x0, local copies, waits for them, and re-layouts: 4.02 us -> none  [the longest x1 1.35 us: fused_body(): pre_gain[None]]
    pallas_call x1 -> x0, Pallas kernels: 3.33 us -> none  [fused_body(): pl.pallas_call(functools.partial(final_kernel, tp), out_shape=jax.ShapeDt...]
    unnamed x0 -> x1, local copies, waits for them, and re-layouts: none -> 2.36 us
where the time goes in v1:
time: 61.8 us; the launch traced here: 61.6 us
  Pallas kernels  58.6 us (95%)
  local copies, waits for them, and re-layouts  2.36 us (4%)
  between operations  0.66 us (1%)
    pallas_call x1, Pallas kernels, fused_body(): pl.pallas_call(functools.partial(main_kernel, (seq, tp, cap, load, quarte...  58.6 us
    unnamed x1, local copies, waits for them, and re-layouts  2.36 us

profile of v1, /device:TPU:0, one launch (start us, length us, event | category | flops | bytes accessed | tf_op | source)
XLA Modules:
  0.0 61.6 jit_solution(4760601502756063158)
XLA Ops:
  0.7 58.6 %shard_map.91 = bf16[128,4608]{1,0:T(8,128)(2,1)} custom-call(s32[1]{0:T(128)S(6)} %copy.11.cnt_ref, s32[1,32]{1,0:T(1,128)} %sel_hbm.1, f32[36,128]{1,0:T(8,128)} %bitcast.3, f32[36,128]{1,0:T(8,128)} %bitcast.4, f32[36,128]{1,0:T(8,128)} %bitcast.5, bf16[128,4608]{1,0:T(8,128)(2,1)} %tok_hbm.1, bf16[4608,1152]{1,0:T(8,128)(2,1)} %gate_hbm.1, ...), custom_call_target="tpu_custom_call" | custom-call | tf_op jit(solution)/shard_map/pallas_call | solution.py:261
  59.3 2.4 %copy.12 = bf16[128,4608]{1,0:T(8,128)(2,1)} copy(bf16[128,4608]{1,0:T(8,128)(2,1)} %shard_map.91) | data formatting | bytes 2359296
